TPU v7x, 8 devices: a whole 2x2x1 slice. The times are simulated.
8 devices in a mesh: rep: 2 (over y, z), dp: 4 (over x, core).
Axes of the slice: x: 2, y: 2, z: 1, core: 2. Of those that a mesh axis runs over, the one named last changes fastest.
Arguments:
- x: bfloat16 [8, 2048, 896], P(('rep', 'dp')), parts along dimension 0
- dy: bfloat16 [8, 2048, 896], P(('rep', 'dp')), parts along dimension 0
- w_gate: bfloat16 [2, 896, 2560], replicated
- w_up: bfloat16 [2, 896, 2560], replicated
- w_down: bfloat16 [2, 2560, 896], replicated
- m_w_gate: float32 [2, 896, 2560], P(None, 'dp')
- m_w_up: float32 [2, 896, 2560], P(None, 'dp')
- m_w_down: float32 [2, 2560, 896], P(None, 'dp')
- v_w_gate: float32 [2, 896, 2560], P(None, 'dp')
- v_w_up: float32 [2, 896, 2560], P(None, 'dp')
- v_w_down: float32 [2, 2560, 896], P(None, 'dp')
Outputs:
- output 1: bfloat16 [4, 896, 2560], P('rep'), parts along dimension 0
- output 2: bfloat16 [4, 896, 2560], P('rep'), parts along dimension 0
- output 3: bfloat16 [4, 2560, 896], P('rep'), parts along dimension 0
- output 4: float32 [4, 896, 2560], P('rep', 'dp'), parts along dimension 0
- output 5: float32 [4, 896, 2560], P('rep', 'dp'), parts along dimension 0
- output 6: float32 [4, 2560, 896], P('rep', 'dp'), parts along dimension 0
- output 7: float32 [4, 896, 2560], P('rep', 'dp'), parts along dimension 0
- output 8: float32 [4, 896, 2560], P('rep', 'dp'), parts along dimension 0
- output 9: float32 [4, 2560, 896], P('rep', 'dp'), parts along dimension 0
There are 2 independent parts. A program takes and returns all parts, laid end to end along the dimension named above; an argument that names none is the same for every part.
All inputs are finite; a program needn't handle non-finite values.
Results may differ from a plain program's by a relative error of at most 0.022.
Values are sent between devices in bfloat16 or wider.
A program may use at most 2 GiB of HBM per device.

v0:
```python
import jax
import jax.numpy as jnp
from jax import lax

NAMES = ("w_gate", "w_up", "w_down")


def matmul(a, w):
    return jnp.dot(a, w, preferred_element_type=jnp.float32).astype(jnp.bfloat16)


def normed(h):
    wide = h.astype(jnp.float32)
    scale = lax.rsqrt(jnp.mean(wide**2, -1, keepdims=True) + 1e-6)
    return (wide * scale).astype(jnp.bfloat16)


def layer(h, w):
    a = normed(h)
    gate = jnp.dot(a, w["w_gate"], preferred_element_type=jnp.float32)
    up = jnp.dot(a, w["w_up"], preferred_element_type=jnp.float32)
    return h + matmul((jax.nn.silu(gate) * up).astype(jnp.bfloat16), w["w_down"])


def adamw(w, m, v, g):
    m = 0.9 * m + 0.1 * g
    v = 0.95 * v + 0.05 * g * g
    step = m * lax.rsqrt(v + 1e-8) + 0.1 * w
    return (w - 0.02 * step).astype(jnp.bfloat16), m, v


def stack(weights, h):
    for number in range(weights["w_gate"].shape[0]):
        h = layer(h, {name: w[number] for name, w in weights.items()})
    return h


def solution(mesh):
    groups = mesh.shape["rep"]

    def step(x, dy, *arrays):
        weights, m, v = (arrays[i : i + 3] for i in (0, 3, 6))
        x, dy = (t.reshape(groups, -1, *t.shape[1:]) for t in (x, dy))

        def of_a_group(x, dy):
            _, back = jax.vjp(lambda w: stack(w, x), dict(zip(NAMES, weights, strict=True)))
            by_weights = back(dy)[0]
            gradients = [by_weights[name].astype(jnp.float32) for name in NAMES]
            new = [adamw(w.astype(jnp.float32), m, v, g) for w, m, v, g in zip(weights, m, v, gradients, strict=True)]
            return tuple(one[which] for which in range(3) for one in new)

        return tuple(t.reshape(-1, *t.shape[2:]) for t in jax.vmap(of_a_group)(x, dy))

    return step
```

profile of v0, /device:TPU:0, one launch (start us, length us, event | category | flops | bytes accessed | tf_op | source)
XLA Modules:
  0.0 876.7 jit_solution(4322205737641405654)
XLA Ops:
  16.1 14.2 %fusion.88 = f32[2048,2560]{1,0:T(8,128)S(1)} fusion(bf16[2,896,2560]{2,1,0:T(8,128)(2,1)} %param, bf16[1,2048,896]{2,1,0:T(8,128)(2,1)} %param.2, f32[2048]{0:T(1024)S(1)} %add_rsqrt_fusion), kind=kOutput, calls=%fused_computation.112 | convolution fusion | flops 9400745984 | bytes 29237248 | tf_op jit(solution)/vmap(jvp())/dot_general | solution.py:20
  30.3 22.5 %fusion.86 = f32[2048,2560]{1,0:T(8,128)} fusion(bf16[2,896,2560]{2,1,0:T(8,128)(2,1)} %param.3, bf16[1,2048,896]{2,1,0:T(8,128)(2,1)} %param.2, f32[2048]{0:T(1024)S(1)} %add_rsqrt_fusion), kind=kOutput, calls=%fused_computation.110 | convolution fusion | flops 9400745984 | bytes 29237248 | tf_op jit(solution)/vmap(jvp())/dot_general | solution.py:21
  52.8 15.4 %fusion.26 = bf16[2048,2560]{1,0:T(8,128)(2,1)} fusion(f32[2048,2560]{1,0:T(8,128)} %fusion.86, f32[2048,2560]{1,0:T(8,128)S(1)} %fusion.88), kind=kLoop, calls=%fused_computation.41 | loop fusion | flops 31457280 | bytes 52428800
  68.3 15.4 %fusion.39 = (f32[2048]{0:T(1024)S(1)}, bf16[1,1,2048,896]{2,3,1,0:T(8,128)(2,1)S(1)}) fusion(bf16[2048,2560]{1,0:T(8,128)(2,1)} %fusion.26, bf16[2,2560,896]{2,1,0:T(8,128)(2,1)} %param.4, bf16[1,2048,896]{1,2,0:T(8,128)(2,1)} %copy), kind=kOutput, calls=%fused_computation.56 | convolution fusion | flops 9404413952 | bytes 22421504 | tf_op jit(solution)/vmap(jvp())/dot_general | solution.py:9
  83.7 18.3 %fusion.75 = f32[2048,2560]{1,0:T(8,128)} fusion(bf16[2,896,2560]{2,1,0:T(8,128)(2,1)} %param, bf16[1,1,2048,896]{2,3,1,0:T(8,128)(2,1)S(1)} %get-tuple-element.10, f32[2048]{0:T(1024)S(1)} %bitcast.349), kind=kOutput, calls=%fused_computation.99 | convolution fusion | flops 9400745984 | bytes 29237248 | tf_op jit(solution)/vmap(jvp())/dot_general | solution.py:20
  102.1 17.4 %fusion.79 = f32[2048,2560]{1,0:T(8,128)} fusion(bf16[2,896,2560]{2,1,0:T(8,128)(2,1)} %param.3, bf16[1,1,2048,896]{2,3,1,0:T(8,128)(2,1)S(1)} %get-tuple-element.10, f32[2048]{0:T(1024)S(1)} %bitcast.350), kind=kOutput, calls=%fused_computation.103 | convolution fusion | flops 9400745984 | bytes 29237248 | tf_op jit(solution)/vmap(jvp())/dot_general | solution.py:21
  119.4 15.6 %convolution_convert_fusion.1 = bf16[2048,2560]{1,0:T(8,128)(2,1)} fusion(bf16[2,2560,896]{2,1,0:T(8,128)(2,1)} %param.4, bf16[1,2048,896]{2,1,0:T(8,128)(2,1)S(1)} %copy-done.2), kind=kOutput, calls=%fused_computation.40 | convolution fusion | flops 9400483840 | bytes 18743296 | tf_op jit(solution)/vmap(transpose(jvp()))/dot_general | solution.py:9
  141.1 22.6 %fusion.6 = bf16[2048,2560]{1,0:T(8,128)(2,1)} fusion(f32[2048,2560]{1,0:T(8,128)} %fusion.75, f32[2048,2560]{1,0:T(8,128)} %fusion.79, bf16[2048,2560]{1,0:T(8,128)(2,1)} %convolution_convert_fusion.1), kind=kLoop, calls=%fused_computation.11 | loop fusion | flops 62914560 | bytes 62914560
  163.7 15.3 %fusion.77 = bf16[2048,896]{0,1:T(8,128)(2,1)} fusion(bf16[2048,2560]{1,0:T(8,128)(2,1)} %fusion.6, bf16[2,896,2560]{2,1,0:T(8,128)(2,1)} %param), kind=kOutput, calls=%fused_computation.101 | convolution fusion | flops 9395240960 | bytes 18743296 | tf_op jit(solution)/vmap(transpose(jvp()))/dot_general | solution.py:20
  179.1 20.5 %fusion.41 = (f32[2048]{0:T(1024)}, bf16[2048,896]{0,1:T(8,128)(2,1)}) fusion(bf16[1,1,2048,896]{2,3,1,0:T(8,128)(2,1)S(1)} %copy-done.4, bf16[2048,896]{0,1:T(8,128)(2,1)} %fusion.77, bf16[2,896,2560]{2,1,0:T(8,128)(2,1)} %param.3, bf16[2048,2560]{1,0:T(8,128)(2,1)} %convolution_convert_fusion.1, f32[2048,2560]{1,0:T(8,128)} %fusion.75), kind=kOutput, calls=%fused_computation.58 | convolution fusion | flops 9437706240 | bytes 47063040 | tf_op jit(solution)/vmap(transpose(jvp()))/dot_general | solution.py:21
  200.3 6.5 fusion.102
  206.9 15.8 %convolution_bitcast_fusion = f32[1,2560,896]{2,1,0:T(8,128)} fusion(bf16[2048,2560]{1,0:T(8,128)(2,1)S(1)} %bitcast.342, bf16[2048,896]{0,1:T(8,128)(2,1)} %fusion.102), kind=kOutput, calls=%fused_computation.67 | convolution fusion | flops 9395240960 | bytes 23330816 | tf_op jit(solution)/vmap(transpose(jvp()))/dot_general | solution.py:9
  222.8 22.0 %fusion.42 = f32[1,2560,896]{2,1,0:T(8,128)} fusion(f32[2048,2560]{1,0:T(8,128)} %fusion.79, f32[2048,2560]{1,0:T(8,128)} %fusion.75, bf16[1,2048,896]{2,1,0:T(8,128)(2,1)} %param.5), kind=kOutput, calls=%fused_computation.63 | convolution fusion | flops 9426698240 | bytes 54788096 | tf_op jit(solution)/vmap(transpose(jvp()))/dot_general | solution.py:9
  244.9 16.7 %convolution_convert_fusion = bf16[2048,2560]{1,0:T(8,128)(2,1)} fusion(bf16[2048,896]{0,1:T(8,128)(2,1)} %fusion.102, bf16[2,2560,896]{2,1,0:T(8,128)(2,1)} %param.4), kind=kOutput, calls=%fused_computation.39 | convolution fusion | flops 9400483840 | bytes 18743296 | tf_op jit(solution)/vmap(transpose(jvp()))/dot_general | solution.py:9
  261.6 19.3 %fusion.51 = f32[1,896,2560]{2,1,0:T(8,128)} fusion(bf16[2048,2560]{1,0:T(8,128)(2,1)} %convolution_convert_fusion, f32[2048,2560]{1,0:T(8,128)} %copy-done, bf16[1,2048,896]{1,2,0:T(8,128)(2,1)} %copy, f32[2048]{0:T(1024)S(1)} %copy-done.8), kind=kOutput, calls=%fused_computation.66 | convolution fusion | flops 9432203264 | bytes 44310528 | tf_op jit(solution)/vmap(transpose(jvp()))/dot_general | solution.py:21
  281.6 19.4 %fusion.45 = f32[1,896,2560]{2,1,0:T(8,128)} fusion(bf16[2048,2560]{1,0:T(8,128)(2,1)} %convolution_convert_fusion.1, f32[2048,2560]{1,0:T(8,128)} %fusion.75, bf16[1,1,2048,896]{2,3,1,0:T(8,128)(2,1)} %copy-done.3, f32[2048]{0:T(1024)S(1)} %bitcast.352), kind=kOutput, calls=%fused_computation.64 | convolution fusion | flops 9432203264 | bytes 44310528 | tf_op jit(solution)/vmap(transpose(jvp()))/dot_general | solution.py:21
  301.1 15.6 %convolution_bitcast_fusion.1 = f32[1,896,2560]{2,1,0:T(8,128)} fusion(bf16[2048,2560]{1,0:T(8,128)(2,1)} %fusion.6, bf16[1,1,2048,896]{2,3,1,0:T(8,128)(2,1)} %copy-done.3, f32[2048]{0:T(1024)S(1)} %bitcast.353), kind=kOutput, calls=%fused_computation.68 | convolution fusion | flops 9400745984 | bytes 23339008 | tf_op jit(solution)/vmap(transpose(jvp()))/dot_general | solution.py:20
  316.8 26.5 %fusion.48 = f32[1,896,2560]{2,1,0:T(8,128)} fusion(f32[2048,2560]{1,0:T(8,128)} %copy-done, f32[2048,2560]{1,0:T(8,128)} %fusion.86, bf16[2048,2560]{1,0:T(8,128)(2,1)} %convolution_convert_fusion, bf16[1,2048,896]{1,2,0:T(8,128)(2,1)} %copy, f32[2048]{0:T(1024)S(1)} %copy-done.8), kind=kOutput, calls=%fused_computation.65 | convolution fusion | flops 9458417664 | bytes 65282048 | tf_op jit(solution)/vmap(transpose(jvp()))/dot_general | solution.py:20
  347.0 21.1 %reduce-scatter.27.cloned.1.call-done = f32[1,640,896]{2,1,0:T(8,128)} async-done(((f32[1,2560,896]{2,1,0:T(8,128)}), f32[1,640,896]{2,1,0:T(8,128)}) %reduce-scatter.27.cloned.1.call-update) | async-done | bytes 2293776
  369.9 8.2 fusion.117
  378.2 63.0 %reduce-scatter.25.cloned.1.call-done = f32[1,224,2560]{2,1,0:T(8,128)} async-done(((f32[1,896,2560]{2,1,0:T(8,128)}), f32[1,224,2560]{2,1,0:T(8,128)}) %reduce-scatter.25.cloned.1.call-update) | async-done | bytes 2293776
  443.0 70.6 %reduce-scatter.23.cloned.1.call-done = f32[1,224,2560]{2,1,0:T(8,128)} async-done(((f32[1,896,2560]{2,1,0:T(8,128)}), f32[1,224,2560]{2,1,0:T(8,128)}) %reduce-scatter.23.cloned.1.call-update) | async-done | bytes 2293776
  515.3 8.2 fusion.118
  523.6 62.9 %reduce-scatter.19.cloned.1.call-done = f32[1,224,2560]{2,1,0:T(8,128)} async-done(((f32[1,896,2560]{2,1,0:T(8,128)}), f32[1,224,2560]{2,1,0:T(8,128)}) %reduce-scatter.19.cloned.1.call-update) | async-done | bytes 2293776
  588.2 71.1 %reduce-scatter.21.cloned.1.call-done = f32[1,224,2560]{2,1,0:T(8,128)} async-done(((f32[1,896,2560]{2,1,0:T(8,128)}), f32[1,224,2560]{2,1,0:T(8,128)}) %reduce-scatter.21.cloned.1.call-update) | async-done | bytes 2293776
  661.1 8.2 fusion.119
  669.3 51.8 %all-gather.14.cloned.1.call-done = bf16[1,2,2560,896]{3,2,1,0:T(8,128)(2,1)} async-done(((bf16[1,2,640,896]{3,2,1,0:T(8,128)(2,1)}), bf16[1,2,2560,896]{3,2,1,0:T(8,128)(2,1)}) %all-gather.14.cloned.1.call-update) | async-done | bytes 9175056 | tf_op jit(solution)/reshape | solution.py:52
  721.2 62.4 %all-gather.12.cloned.1.call-done = bf16[1,2,896,2560]{3,2,1,0:T(8,128)(2,1)} async-done(((bf16[1,2,224,2560]{3,2,1,0:T(8,128)(2,1)}), bf16[1,2,896,2560]{3,2,1,0:T(8,128)(2,1)}) %all-gather.12.cloned.1.call-update) | async-done | bytes 9175056 | tf_op jit(solution)/reshape | solution.py:52
  783.6 62.4 %all-gather.10.cloned.1.call-done = bf16[1,2,896,2560]{3,2,1,0:T(8,128)(2,1)} async-done(((bf16[1,2,224,2560]{3,2,1,0:T(8,128)(2,1)}), bf16[1,2,896,2560]{3,2,1,0:T(8,128)(2,1)}) %all-gather.10.cloned.1.call-update) | async-done | bytes 9175056 | tf_op jit(solution)/reshape | solution.py:52
  846.0 7.9 copy.5
  853.9 7.8 copy.6
  861.7 8.0 copy.7
  (60 shorter events, 28.6 us)
Async XLA Ops:
  7.2 338.0 %reduce-scatter.29.cloned.1.call-start = ((), (), s32[]{:S(2)}) async-start(), calls=%async_computation.14 | async-start | bytes 11468800
  16.1 14.2 %copy-start.7 = (f32[2048]{0:T(1024)}, f32[2048]{0:T(1024)S(1)}, u32[]{:S(2)}) copy-start(f32[2048]{0:T(1024)S(1)} %add_rsqrt_fusion) | copy-start | bytes 24580
  30.3 22.5 %copy-start = (f32[2048,2560]{1,0:T(8,128)}, f32[2048,2560]{1,0:T(8,128)S(1)}, u32[]{:S(2)}) copy-start(f32[2048,2560]{1,0:T(8,128)S(1)} %fusion.88) | copy-start | bytes 62914564
  83.7 18.4 %copy-start.3 = (bf16[1,1,2048,896]{2,3,1,0:T(8,128)(2,1)}, bf16[1,1,2048,896]{2,3,1,0:T(8,128)(2,1)S(1)}, u32[]{:S(2)}) copy-start(bf16[1,1,2048,896]{2,3,1,0:T(8,128)(2,1)S(1)} %get-tuple-element.10) | copy-start | bytes 11010052
  83.7 18.4 %copy-start.5 = (f32[1,1,2048]{2,1,0:T(1,128)}, f32[1,1,2048]{2,1,0:T(1,128)S(1)}, u32[]{:S(2)}) copy-start(f32[1,1,2048]{2,1,0:T(1,128)S(1)} %rsqrt.31) | copy-start | bytes 24580
  102.1 17.4 %copy-start.2 = (bf16[1,2048,896]{2,1,0:T(8,128)(2,1)S(1)}, bf16[1,2048,896]{2,1,0:T(8,128)(2,1)}, u32[]{:S(2)}) copy-start(bf16[1,2048,896]{2,1,0:T(8,128)(2,1)} %param.5) | copy-start | bytes 11010052
  163.7 15.3 %copy-start.4 = (bf16[1,1,2048,896]{2,3,1,0:T(8,128)(2,1)S(1)}, bf16[1,1,2048,896]{2,3,1,0:T(8,128)(2,1)}, u32[]{:S(2)}) copy-start(bf16[1,1,2048,896]{2,3,1,0:T(8,128)(2,1)} %copy-done.3) | copy-start | bytes 11010052
  163.7 43.2 %slice-start = ((s8[10485760]{0:T(1024)(128)(4,1)}), s8[4194304]{0:T(1024)(128)(4,1)S(1)}, s32[]{:S(2)}) async-start(s8[10485760]{0:T(1024)(128)(4,1)} %bitcast.341), calls=%async_computation.15 | async-start | bytes 8388608
  179.0 21.3 %copy-start.1 = (bf16[1,2048,896]{1,2,0:T(8,128)(2,1)S(1)}, bf16[1,2048,896]{1,2,0:T(8,128)(2,1)}, u32[]{:S(2)}) copy-start(bf16[1,2048,896]{1,2,0:T(8,128)(2,1)} %copy.1) | copy-start | bytes 11010052
  179.0 27.8 %slice-start.1 = ((s8[10485760]{0:T(1024)(128)(4,1)}), s8[4194304]{0:T(1024)(128)(4,1)S(1)}, s32[]{:S(2)}) async-start(s8[10485760]{0:T(1024)(128)(4,1)} %bitcast.341), calls=%async_computation.16 | async-start | bytes 8388608
  179.0 27.8 %slice-start.2 = ((s8[10485760]{0:T(1024)(128)(4,1)}), s8[2097152]{0:T(1024)(128)(4,1)S(1)}, s32[]{:S(2)}) async-start(s8[10485760]{0:T(1024)(128)(4,1)} %bitcast.341), calls=%async_computation.17 | async-start | bytes 4194304
  222.8 145.3 %reduce-scatter.27.cloned.1.call-start = ((), (), s32[]{:S(2)}) async-start(), calls=%async_computation.13 | async-start | bytes 11468800
  244.8 16.8 %copy-start.8 = (f32[2048]{0:T(1024)S(1)}, f32[2048]{0:T(1024)}, u32[]{:S(2)}) copy-start(f32[2048]{0:T(1024)} %copy-done.7) | copy-start | bytes 24580
  244.9 196.3 %reduce-scatter.25.cloned.1.call-start = ((), (), s32[]{:S(2)}) async-start(), calls=%async_computation.12 | async-start | bytes 11468800
  280.9 0.7 copy-start.6
  281.0 232.6 %reduce-scatter.23.cloned.1.call-start = ((), (), s32[]{:S(2)}) async-start(), calls=%async_computation.11 | async-start | bytes 11468800
  301.0 285.4 %reduce-scatter.19.cloned.1.call-start = ((), (), s32[]{:S(2)}) async-start(), calls=%async_computation.9 | async-start | bytes 11468800
  316.7 342.6 %reduce-scatter.21.cloned.1.call-start = ((), (), s32[]{:S(2)}) async-start(), calls=%async_computation.10 | async-start | bytes 11468800
  343.3 0.7 copy-start.9
  343.3 377.9 %all-gather.14.cloned.1.call-start = ((), (), s32[]{:S(2)}) async-start(), calls=%async_computation.8 | async-start | bytes 11468800 | tf_op jit(solution)/reshape | solution.py:52
  378.1 405.4 %all-gather.12.cloned.1.call-start = ((), (), s32[]{:S(2)}) async-start(), calls=%async_computation.7 | async-start | bytes 11468800 | tf_op jit(solution)/reshape | solution.py:52
  523.5 322.5 %all-gather.10.cloned.1.call-start = ((), (), s32[]{:S(2)}) async-start(), calls=%async_computation.6 | async-start | bytes 11468800 | tf_op jit(solution)/reshape | solution.py:52
Sparse Core Ops, SparseCore 0:
  222.9 72.6 reduce-scatter.28
  298.2 69.8 reduce-scatter.26
  371.3 69.8 reduce-scatter.24
  443.6 69.8 reduce-scatter.22
  516.5 69.8 reduce-scatter.18
  589.4 69.8 reduce-scatter.20
  660.9 60.2 all-gather.13
  723.3 60.2 all-gather.11
  785.7 60.2 all-gather.9
where the time goes:
time: 886 us; the launch traced here: 877 us
  waiting for transfers between devices  466 us (53%)
  matrix products  275 us (31%)
  other arithmetic  83.4 us (9%)
  local copies, waits for them, and re-layouts  37.7 us (4%)
  between operations  15.1 us (2%)
    unnamed x15, waiting for transfers between devices  289 us
    reshape x3, waiting for transfers between devices, step(): t.reshape(-1, *t.shape[2:])  177 us
    dot_general x5, matrix products, layer(): up = jnp.dot(a, w['w_up'], preferred_element_type=jnp.float32)  99.1 us
    dot_general x5, matrix products, layer(): gate = jnp.dot(a, w['w_gate'], preferred_element_type=jnp.float32)  89.9 us
    dot_general x5, matrix products, matmul(): jnp.dot(a, w, preferred_element_type=jnp.float32).astype(jnp.bfloat16)  85.6 us
    unnamed x4, other arithmetic  44.6 us
    unnamed x31, local copies, waits for them, and re-layouts  37.1 us
    reshape x3, other arithmetic, step(): t.reshape(-1, *t.shape[2:])  24.6 us
  transfers between devices with their start and end apart: 9, of which 8 were waited for; matrix products, arithmetic and copies ran while one was open for 18% of the time, Pallas kernels for 0%

commit v1 on v0

v1 whole, which is shorter than its diff:
```python
import functools

import jax
import jax.numpy as jnp
from jax import lax
from jax.experimental import pallas as pl
from jax.experimental.pallas import tpu as pltpu

T, D, FF, LAYERS = 2048, 896, 2560, 2
LANES = 128
STRIPES, CHUNKS = 4, 5
CH = STRIPES * LANES
QD, QF = D // 4, FF // 4
TM = 256
TILES = T // TM
PACK = (3, D, LANES)
ANY = pl.BlockSpec(memory_space=pl.ANY)
VMEM = pl.BlockSpec(memory_space=pltpu.VMEM)
BF, F32 = jnp.bfloat16, jnp.float32
TOKEN = jax.ShapeDtypeStruct((8, LANES), F32)
LIMIT = 60 * 1024 * 1024


def shape(*dims, dtype=BF):
    return jax.ShapeDtypeStruct(dims, dtype)


def dot(a, b):
    return jnp.dot(a, b, preferred_element_type=F32)


def dot_nt(a, b):
    return lax.dot_general(a, b, (((1,), (1,)), ((), ())), preferred_element_type=F32)


def sigmoid(g):
    return 0.5 * jnp.tanh(0.5 * g) + 0.5


def scale_of(wide):
    return lax.rsqrt(jnp.mean(wide * wide, -1, keepdims=True) + 1e-6)


def rows(t, size=TM):
    return pl.ds(pl.multiple_of(t * size, size), size)


def params(**kw):
    return pltpu.CompilerParams(vmem_limit_bytes=LIMIT, **kw)


def cost(flops, nbytes):
    return pl.CostEstimate(flops=int(flops), bytes_accessed=int(nbytes), transcendentals=0)


MATMUL = 2 * T * D * FF


def forward_kernel(x_ref, dy_ref, wg_ref, wu_ref, wd_ref, h_out, a_out, at_out, dyt_out, tok, a0, acc, h_v, a_v, at_v, dyt_v, sems):
    j = pl.program_id(0)

    @pl.when(j == 0)
    def _():
        def body(t, _):
            wide = x_ref[0, rows(t), :].astype(F32)
            a0[rows(t), :] = (wide * scale_of(wide)).astype(BF)
            return 0

        lax.fori_loop(0, TILES, body, 0)

    def tile(t, first, last):
        g = dot(a0[rows(t), :], wg_ref[0])
        u = dot(a0[rows(t), :], wu_ref[0])
        z = (g * sigmoid(g) * u).astype(BF)
        part = dot(z, wd_ref[0])
        if first:
            acc[rows(t), :] = part
        elif not last:
            acc[rows(t), :] += part
        else:
            h = x_ref[0, rows(t), :] + (acc[rows(t), :] + part).astype(BF)
            h_v[rows(t), :] = h
            wide = h.astype(F32)
            a = (wide * scale_of(wide)).astype(BF)
            a_v[rows(t), :] = a
            at_v[:, rows(t)] = a.T
            for i, (src, dst) in enumerate(((h_v, h_out), (a_v, a_out))):
                pltpu.make_async_copy(src.at[rows(t)], dst.at[rows(t)], sems.at[i, t]).start()
            pltpu.make_async_copy(at_v.at[:, rows(t)], at_out.at[:, rows(t)], sems.at[2, t]).start()

    @pl.when(j == 0)
    def _():
        lax.fori_loop(0, TILES, lambda t, _: (tile(t, True, False), 0)[1], 0)

    @pl.when((j > 0) & (j < CHUNKS - 1))
    def _():
        lax.fori_loop(0, TILES, lambda t, _: (tile(t, False, False), 0)[1], 0)

    @pl.when(j == 1)
    def _():
        def body(t, _):
            dyt_v[:, rows(t)] = dy_ref[0, rows(t), :].T
            pltpu.make_async_copy(dyt_v.at[:, rows(t)], dyt_out.at[:, rows(t)], sems.at[3, t]).start()
            return 0

        lax.fori_loop(0, TILES, body, 0)

    @pl.when(j == CHUNKS - 1)
    def _():
        lax.fori_loop(0, TILES, lambda t, _: (tile(t, False, True), 0)[1], 0)

        def finish(t, _):
            for i, (src, dst) in enumerate(((h_v, h_out), (a_v, a_out))):
                pltpu.make_async_copy(src.at[rows(t)], dst.at[rows(t)], sems.at[i, t]).wait()
            pltpu.make_async_copy(at_v.at[:, rows(t)], at_out.at[:, rows(t)], sems.at[2, t]).wait()
            pltpu.make_async_copy(dyt_v.at[:, rows(t)], dyt_out.at[:, rows(t)], sems.at[3, t]).wait()
            return 0

        lax.fori_loop(0, TILES, finish, 0)


def forward(x, dy, wg, wu, wd):
    whole = pl.BlockSpec((1, T, D), lambda j: (0, 0, 0), pipeline_mode=pl.Buffered(1))
    return pl.pallas_call(
        forward_kernel,
        grid=(CHUNKS,),
        in_specs=[
            whole,
            whole,
            pl.BlockSpec((1, D, CH), lambda j: (0, 0, j)),
            pl.BlockSpec((1, D, CH), lambda j: (0, 0, j)),
            pl.BlockSpec((1, CH, D), lambda j: (0, j, 0)),
        ],
        out_specs=[ANY] * 5,
        out_shape=[shape(T, D), shape(T, D), shape(D, T), shape(D, T), TOKEN],
        scratch_shapes=[
            pltpu.VMEM((T, D), BF),
            pltpu.VMEM((T, D), F32),
            pltpu.VMEM((T, D), BF),
            pltpu.VMEM((T, D), BF),
            pltpu.VMEM((D, T), BF),
            pltpu.VMEM((D, T), BF),
            pltpu.SemaphoreType.DMA((4, TILES)),
        ],
        compiler_params=params(dimension_semantics=("arbitrary",)),
        cost_estimate=cost(3 * MATMUL, 30e6),
        name="forward_0",
    )(x, dy, wg, wu, wd)


def chunk_kernel(layer, j, keep_d, *refs):
    a_in, at_in, d_in, dt_in, wg_in, wu_in, wd_in = refs[:7]
    refs = refs[8 + (2 if keep_d == 2 else 0) :]
    if keep_d:
        send, keep, dg_out, du_out, tok = refs[:5]
        refs = refs[5:]
    else:
        send, keep, tok = refs[:3]
        refs = refs[3:]
    a, at, d, dt, wg, wu, wd, z, dg, du, both, sems, tile_sems = refs
    me = lax.axis_index("dp")
    chip, core = me // 2, me % 2

    loads = []
    for p in range(STRIPES):
        cols = pl.ds(QF * p + LANES * j, LANES)
        at_p = pl.ds(LANES * p, LANES)
        loads.append((wg_in.at[layer, :, cols], wg.at[:, at_p]))
        loads.append((wu_in.at[layer, :, cols], wu.at[:, at_p]))
        loads.append((wd_in.at[layer, cols, :], wd.at[at_p, :]))
    loads = [pltpu.make_async_copy(s, t, sems.at[i]) for i, (s, t) in enumerate(loads)]
    for copy in loads:
        copy.start()
    tiles = [[pltpu.make_async_copy(s.at[pl.ds(TM * t, TM)], v.at[pl.ds(TM * t, TM)], tile_sems.at[i, t]) for i, (s, v) in enumerate(((a_in, a), (d_in, d)))] for t in range(TILES)]
    for pair in tiles:
        for copy in pair:
            copy.start()
    n = len(loads)
    late = [pltpu.make_async_copy(dt_in, dt, sems.at[n]), pltpu.make_async_copy(at_in, at, sems.at[n + 1])]
    for copy in late:
        copy.start()
    for copy in loads:
        copy.wait()

    def first(t, _):
        for i, (s, v) in enumerate(((a_in, a), (d_in, d))):
            pltpu.make_async_copy(s.at[rows(t)], v.at[rows(t)], tile_sems.at[i, t]).wait()
        g = dot(a[rows(t), :], wg[...])
        u = dot(a[rows(t), :], wu[...])
        dz = dot_nt(d[rows(t), :], wd[...]).astype(BF).astype(F32)
        s = sigmoid(g)
        silu = g * s
        z[rows(t), :] = (silu * u).astype(BF)
        du[rows(t), :] = (dz * silu).astype(BF)
        dg[rows(t), :] = (dz * u * (s + silu * (1 - s))).astype(BF)
        return 0

    lax.fori_loop(0, TILES, first, 0)

    stores = []
    if keep_d:
        for p in range(STRIPES):
            cols = pl.ds(QF * p + LANES * j, LANES)
            at_p = pl.ds(LANES * p, LANES)
            stores.append(pltpu.make_async_copy(dg.at[:, at_p], dg_out.at[:, cols], sems.at[n + 2 + 2 * p]))
            stores.append(pltpu.make_async_copy(du.at[:, at_p], du_out.at[:, cols], sems.at[n + 3 + 2 * p]))
        for copy in stores:
            copy.start()

    def place(q):
        return (q % 2) ^ core, (q // 2) ^ chip

    late[0].wait()

    def down(b0, size):
        r = dot(dt[pl.ds(b0, size), :], z[...])
        for p in range(STRIPES):
            side, rel = place(p)
            for i in range(size // LANES):
                block = r[LANES * i : LANES * (i + 1), LANES * p : LANES * (p + 1)].T.astype(BF)
                both[side, rel, 2, pl.ds(b0 + LANES * i, LANES), :] = block

    lax.fori_loop(0, 3, lambda b, _: (down(pl.multiple_of(b * 256, 256), 256), 0)[1], 0)
    down(768, 128)
    late[1].wait()

    def gate_up(q, _):
        side, rel = place(q)
        for i, grad in enumerate((dg, du)):
            r = dot(at[pl.ds(pl.multiple_of(q * QD, 32), QD), :], grad[...]).astype(BF)
            for p in range(STRIPES):
                both[side, rel, i, QD * p : QD * (p + 1), :] = r[:, LANES * p : LANES * (p + 1)]
        return 0

    lax.fori_loop(0, 4, gate_up, 0)
    k = n + 2 + 2 * STRIPES
    out = [pltpu.make_async_copy(both.at[1], send, sems.at[k]), pltpu.make_async_copy(both.at[0], keep, sems.at[k + 1])]
    for copy in out:
        copy.start()
    for copy in out + stores:
        copy.wait()


def chunk(layer, j, a, at, d, dt, w, tok, kept=None, keep_d=False):
    mode = 0 if not keep_d else (1 if kept is None else 2)
    out_shape = [shape(2, *PACK), shape(2, *PACK)]
    if mode:
        out_shape += [shape(T, FF), shape(T, FF)]
    extra = list(kept) if mode == 2 else []
    return pl.pallas_call(
        functools.partial(chunk_kernel, layer, j, mode),
        in_specs=[ANY] * (8 + len(extra)),
        out_specs=[ANY] * (len(out_shape) + 1),
        out_shape=out_shape + [TOKEN],
        input_output_aliases={8: 2, 9: 3} if mode == 2 else {},
        scratch_shapes=[
            pltpu.VMEM((T, D), BF),
            pltpu.VMEM((D, T), BF),
            pltpu.VMEM((T, D), BF),
            pltpu.VMEM((D, T), BF),
            pltpu.VMEM((D, CH), BF),
            pltpu.VMEM((D, CH), BF),
            pltpu.VMEM((CH, D), BF),
            pltpu.VMEM((T, CH), BF),
            pltpu.VMEM((T, CH), BF),
            pltpu.VMEM((T, CH), BF),
            pltpu.VMEM((2, 2, *PACK), BF),
            pltpu.SemaphoreType.DMA((3 * STRIPES + 4 + 2 * STRIPES,)),
            pltpu.SemaphoreType.DMA((2, TILES)),
        ],
        compiler_params=params(),
        cost_estimate=cost(6 * MATMUL / CHUNKS, 20e6),
        name=f"chunk_{layer}_{j}",
    )(a, at, d, dt, *w, tok, *extra)


def states_kernel(dg, du, wg, wu, h, dy, x, tok_in, dh_out, dht_out, a0_out, a0t_out, tok):
    da = dot_nt(dg[...], wg[0]) + dot_nt(du[...], wu[0])
    da = da.astype(BF).astype(F32)
    wide = h[...].astype(F32)
    s = scale_of(wide)
    along = jnp.sum(da * wide, -1, keepdims=True) * (s * s * s / D)
    dh = dy[0] + (da * s - wide * along).astype(BF)
    dh_out[...] = dh
    dht_out[...] = dh.T
    wide = x[0].astype(F32)
    a0 = (wide * scale_of(wide)).astype(BF)
    a0_out[...] = a0
    a0t_out[...] = a0.T


def states(dg, du, wg, wu, h, dy, x, tok):
    by_row = lambda n: pl.BlockSpec((TM, n), lambda t: (t, 0))
    by_row3 = pl.BlockSpec((1, TM, D), lambda t: (0, t, 0))
    by_col = pl.BlockSpec((D, TM), lambda t: (0, t))
    weight = pl.BlockSpec((1, D, FF), lambda t: (1, 0, 0), pipeline_mode=pl.Buffered(1))
    return pl.pallas_call(
        states_kernel,
        grid=(TILES,),
        in_specs=[by_row(FF), by_row(FF), weight, weight, by_row(D), by_row3, by_row3, ANY],
        out_specs=[by_row(D), by_col, by_row(D), by_col, ANY],
        out_shape=[shape(T, D), shape(D, T), shape(T, D), shape(D, T), TOKEN],
        compiler_params=params(dimension_semantics=("arbitrary",)),
        cost_estimate=cost(2 * MATMUL, 50e6),
        name="states_1",
    )(dg, du, wg, wu, h, dy, x, tok)


def add_kernel(keep, got, tok_in, out, tok):
    out[...] = (keep[0].astype(F32) + got[0].astype(F32)).astype(BF)


def add(keep, got, tok):
    second = pl.BlockSpec((1, *PACK), lambda i: (1, 0, 0, 0))
    return pl.pallas_call(
        add_kernel,
        grid=(1,),
        in_specs=[second, second, ANY],
        out_specs=[pl.BlockSpec(PACK, lambda i: (0, 0, 0)), ANY],
        out_shape=[shape(*PACK), TOKEN],
        compiler_params=params(),
        cost_estimate=cost(2e9, 3e6),
        name="chip_sum",
    )(keep, got, tok)


def blocks(layer, j, owner_rows, owner_hidden):
    for which in range(2):
        for p in range(STRIPES):
            yield which, (layer, owner_rows, pl.ds(QF * p + LANES * j, LANES)), QD * p, QD
    for b in range(D // LANES):
        yield 2, (layer, owner_hidden, pl.ds(LANES * b, LANES)), LANES * b, LANES


def adamw_kernel(layer, j, aliased, *refs):
    keep, got, across = refs[:3]
    w_in, m_in, v_in = refs[3:6], refs[6:9], refs[9:12]
    refs = refs[13 + (6 if aliased else 0) :]
    new_w, m_out, v_out = refs[0], refs[1:4], refs[4:7]
    w, m, v, sems = refs[8:]
    me = lax.axis_index("dp")
    mine = list(blocks(layer, j, pl.ds(0, QD), pl.ds(LANES * j, LANES)))
    whole = list(
        blocks(
            layer,
            j,
            pl.ds(pl.multiple_of(QD * me, 32), QD),
            pl.ds(pl.multiple_of(QF * me + LANES * j, LANES), LANES),
        )
    )
    loads = []
    for i, ((which, at, row, size), (_, at_whole, _, _)) in enumerate(zip(mine, whole)):
        to = (which, pl.ds(row, size))
        loads.append(
            [
                pltpu.make_async_copy(w_in[which].at[at_whole], w.at[to], sems.at[0, i]),
                pltpu.make_async_copy(m_in[which].at[at], m.at[to], sems.at[1, i]),
                pltpu.make_async_copy(v_in[which].at[at], v.at[to], sems.at[2, i]),
            ]
        )
        for copy in loads[-1]:
            copy.start()
    stores = []
    for i, (which, at, row, size) in enumerate(mine):
        for copy in loads[i]:
            copy.wait()
        part = (which, pl.ds(row, size))
        g = keep[0, which, row : row + size].astype(F32) + got[0, which, row : row + size].astype(F32)
        g = (g + across[which, row : row + size].astype(F32)).astype(BF).astype(F32)
        m_new = 0.9 * m[part] + 0.1 * g
        v_new = 0.95 * v[part] + 0.05 * g * g
        wide = w[part].astype(F32)
        step = m_new * lax.rsqrt(v_new + 1e-8) + 0.1 * wide
        new_w[part] = (wide - 0.02 * step).astype(BF)
        m[part] = m_new
        v[part] = v_new
        stores.append(pltpu.make_async_copy(m.at[part], m_out[which].at[at], sems.at[3, i]))
        stores.append(pltpu.make_async_copy(v.at[part], v_out[which].at[at], sems.at[4, i]))
        for copy in stores[-2:]:
            copy.start()
    for copy in stores:
        copy.wait()


def adamw(layer, j, keep, got, across, w, m, v, tok, so_far):
    first = pl.BlockSpec((1, *PACK), lambda i: (0, 0, 0, 0))
    packed = pl.BlockSpec(PACK, lambda i: (0, 0, 0))
    aliased = so_far is not None
    extra = list(so_far) if aliased else []
    n = 3 * STRIPES + D // LANES
    out = pl.pallas_call(
        functools.partial(adamw_kernel, layer, j, aliased),
        grid=(1,),
        in_specs=[first, first, packed] + [ANY] * (10 + len(extra)),
        out_specs=[packed] + [ANY] * 7,
        out_shape=[shape(*PACK)] + [jax.ShapeDtypeStruct(t.shape, t.dtype) for t in (*m, *v)] + [TOKEN],
        input_output_aliases={13 + i: 1 + i for i in range(6)} if aliased else {},
        scratch_shapes=[pltpu.VMEM(PACK, BF), pltpu.VMEM(PACK, F32), pltpu.VMEM(PACK, F32), pltpu.SemaphoreType.DMA((5, n))],
        compiler_params=params(),
        cost_estimate=cost(4e9, 8e6),
        name=f"adamw_{layer}_{j}",
    )(keep, got, across, *w, *m, *v, tok, *extra)
    return out[0], tuple(out[1:7]), out[7]


def place_kernel(layer, j, aliased, *refs):
    parts = refs[:4]
    refs = refs[5 + (3 if aliased else 0) :]
    outs, sems = refs[:3], refs[4]
    me = lax.axis_index("dp")
    chip, core = me // 2, me % 2
    copies = []
    for k, (part, rel_chip, rel_core) in enumerate(zip(parts, (0, 1, 0, 1), (0, 0, 1, 1))):
        q = (chip ^ rel_chip) * 2 + (core ^ rel_core)
        where = blocks(layer, j, pl.ds(pl.multiple_of(QD * q, 32), QD), pl.ds(pl.multiple_of(QF * q + LANES * j, LANES), LANES))
        for i, (which, at, row, size) in enumerate(where):
            copies.append(pltpu.make_async_copy(part.at[which, pl.ds(row, size)], outs[which].at[at], sems.at[k, i]))
            copies[-1].start()
    for copy in copies:
        copy.wait()


def place(layer, j, parts, w, tok, so_far):
    aliased = so_far is not None
    extra = list(so_far) if aliased else []
    n = 2 * STRIPES + D // LANES
    out = pl.pallas_call(
        functools.partial(place_kernel, layer, j, aliased),
        in_specs=[VMEM] * 4 + [ANY] * (1 + len(extra)),
        out_specs=[ANY] * 4,
        out_shape=[jax.ShapeDtypeStruct(t.shape, t.dtype) for t in w] + [TOKEN],
        input_output_aliases={5 + i: i for i in range(3)} if aliased else {},
        scratch_shapes=[pltpu.SemaphoreType.DMA((4, n))],
        compiler_params=params(),
        cost_estimate=cost(2e9, 6e6),
        name=f"place_{layer}_{j}",
    )(*parts, tok, *extra)
    return tuple(out[:3]), out[3]


ORDER = (
    "C10 S10 C11 S11 C12 S12 A10 C13 S13 A11 C14 S14 A12 D A13 C00 S00 A14 P10 C01 S01 P11 C02 S02 A00 P12"
    " C03 S03 A01 P13 C04 S04 A02 P14 A03 P00 A04 P01 P02 P03 P04"
).split()


def solution(mesh):
    from jax.sharding import PartitionSpec as P

    across = [(i, i ^ 2) for i in range(4)]
    partner = [(i, i ^ 1) for i in range(4)]

    def step(x, dy, wg, wu, wd, *moments):
        w, m, v = (wg, wu, wd), moments[:3], moments[3:]
        h, a1, a1t, dyt, tok = forward(x, dy, wg, wu, wd)
        dy2 = dy.reshape(T, D)
        inputs = {1: (a1, a1t, dy2, dyt)}
        kept, mv, new = None, None, None
        keep, got, crossed, parts = {}, {}, {}, {}
        for name in ORDER:
            kind, key = name[0], tuple(int(i) for i in name[1:])
            if kind == "C":
                layer, j = key
                if layer:
                    send, keep[key], *kept, tok = chunk(layer, j, *inputs[layer], w, tok, kept, True)
                else:
                    send, keep[key], tok = chunk(layer, j, *inputs[layer], w, tok)
                got[key] = lax.ppermute(send, "dp", partner)
            elif kind == "S":
                total, tok = add(keep[key], got[key], tok)
                crossed[key] = lax.ppermute(total, "dp", across)
            elif kind == "A":
                own, mv, tok = adamw(*key, keep[key], got[key], crossed[key], w, m, v, tok, mv)
                other = lax.ppermute(own, "dp", across)
                parts[key] = (own, other, lax.ppermute(own, "dp", partner), lax.ppermute(other, "dp", partner))
            elif kind == "P":
                new, tok = place(*key, parts[key], w, tok, new)
            else:
                dh, dht, a0, a0t, tok = states(*kept, wg, wu, h, dy, x, tok)
                inputs[0] = (a0, a0t, dh, dht)
        return (*new, *mv)

    whole, shard = P(), P(None, "dp")
    return jax.shard_map(
        step,
        mesh=mesh,
        in_specs=(P(("rep", "dp")),) * 2 + (whole,) * 3 + (shard,) * 6,
        out_specs=(P("rep"),) * 3 + (P("rep", "dp"),) * 6,
        check_vma=False,
    )
```

time: 886 us -> 718 us (0.81)
  Pallas kernels: 0 us -> 423 us
  matrix products: 275 us -> 0 us
  waiting for transfers between devices: 466 us -> 232 us
  other arithmetic: 83.4 us -> 0 us
  starting transfers between devices: 0.37 us -> 30 us
  local copies, waits for them, and re-layouts: 37.7 us -> 22.3 us
  between operations: 15.1 us -> 1.89 us
    pallas_call x0 -> x42, Pallas kernels: none -> 423 us  [the longest x10 213 us: chunk(): pl.pallas_call(functools.partial(chunk_kernel, layer, j, mode), in_specs=...]
    unnamed x15 -> x0, waiting for transfers between devices: 289 us -> none
    dot_general x15 -> x0, matrix products: 275 us -> none  [the longest x5 99.1 us: layer(): up = jnp.dot(a, w['w_up'], preferred_element_type=jnp.float32)]
    ppermute x0 -> x50, waiting for transfers between devices: none -> 232 us  [the longest x10 142 us: step(): other = lax.ppermute(own, 'dp', across)]
    reshape x3 -> x0, waiting for transfers between devices: 177 us -> none  [step(): t.reshape(-1, *t.shape[2:])]
    unnamed x4 -> x0, other arithmetic: 44.6 us -> none
    ppermute x0 -> x50, starting transfers between devices: none -> 30 us  [the longest x10 15.2 us: step(): other = lax.ppermute(own, 'dp', across)]
    reshape x3 -> x0, other arithmetic: 24.6 us -> none  [step(): t.reshape(-1, *t.shape[2:])]
  transfers between devices with their start and end apart: 9 -> 50, of which waited for: 8 -> 24; matrix products, arithmetic and copies ran while one was open for 18% -> 0% of each run, Pallas kernels for 0% -> 16%
where the time goes in v1:
time: 718 us; the launch traced here: 709 us
  Pallas kernels  423 us (59%)
  waiting for transfers between devices  232 us (32%)
  starting transfers between devices  30 us (4%)
  local copies, waits for them, and re-layouts  22.3 us (3%)
    pallas_call x10, Pallas kernels, chunk(): pl.pallas_call(functools.partial(chunk_kernel, layer, j, mode), in_specs=...  213 us
    ppermute x10, waiting for transfers between devices, step(): other = lax.ppermute(own, 'dp', across)  142 us
    ppermute x10, waiting for transfers between devices, step(): crossed[key] = lax.ppermute(total, 'dp', across)  81.8 us
    pallas_call x10, Pallas kernels, adamw(): pl.pallas_call(functools.partial(adamw_kernel, layer, j, aliased), grid=(...  62.4 us
    pallas_call x1, Pallas kernels, forward(): pl.pallas_call(forward_kernel, grid=(CHUNKS,), in_specs=[whole, whole, pl...  53.3 us
    pallas_call x10, Pallas kernels, place(): pl.pallas_call(functools.partial(place_kernel, layer, j, aliased), in_spe...  37.8 us
    pallas_call x1, Pallas kernels, states(): pl.pallas_call(states_kernel, grid=(TILES,), in_specs=[by_row(FF), by_row...  32.7 us
    pallas_call x10, Pallas kernels, add(): pl.pallas_call(add_kernel, grid=(1,), in_specs=[second, second, ANY], out...  23.2 us
  transfers between devices with their start and end apart: 50, of which 24 were waited for; matrix products, arithmetic and copies ran while one was open for 0% of the time, Pallas kernels for 16%

profile of v1, /device:TPU:0, one launch (start us, length us, event | category | flops | bytes accessed | tf_op | source)
XLA Modules:
  0.0 709.2 jit_solution(5204948283150969656)
XLA Ops:
  0.6 53.3 %forward_0.1 = (bf16[2048,896]{1,0:T(8,128)(2,1)}, bf16[2048,896]{1,0:T(8,128)(2,1)}, bf16[896,2048]{1,0:T(8,128)(2,1)}, bf16[896,2048]{1,0:T(8,128)(2,1)}, f32[8,128]{1,0:T(8,128)}) custom-call(bf16[1,2048,896]{2,1,0:T(8,128)(2,1)} %x.1, bf16[1,2048,896]{2,1,0:T(8,128)(2,1)} %dy.1, bf16[2,896,2560]{2,1,0:T(8,128)(2,1)} %refs_3_.19, ...), custom_call_target="tpu_custom_call" | custom-call | flops 28185722880 | bytes 30000000 | tf_op jit(solution)/shard_map/forward_0/pallas_call | solution.py:124
  53.9 21.2 %chunk_1_0.1 = (bf16[2,3,896,128]{3,2,1,0:T(8,128)(2,1)}, bf16[2,3,896,128]{3,2,1,0:T(8,128)(2,1)}, bf16[2048,2560]{1,0:T(8,128)(2,1)}, bf16[2048,2560]{1,0:T(8,128)(2,1)}, f32[8,128]{1,0:T(8,128)}) custom-call(bf16[2048,896]{1,0:T(8,128)(2,1)} %get-tuple-element.198.refs_0_, bf16[896,2048]{1,0:T(8,128)(2,1)} %get-tuple-element.199.refs_1_, ...), custom_call_target="tpu_custom_call" | custom-call | flops 11274289152 | bytes 20000000 | tf_op jit(solution)/shard_map/chunk_1_0/pallas_call | solution.py:250
  82.2 21.2 %chunk_1_1.1 = (bf16[2,3,896,128]{3,2,1,0:T(8,128)(2,1)}, bf16[2,3,896,128]{3,2,1,0:T(8,128)(2,1)}, bf16[2048,2560]{1,0:T(8,128)(2,1)}, bf16[2048,2560]{1,0:T(8,128)(2,1)}, f32[8,128]{1,0:T(8,128)}) custom-call(bf16[2048,896]{1,0:T(8,128)(2,1)} %get-tuple-element.198.refs_0_, ...), custom_call_target="tpu_custom_call", output_to_operand_aliasing={{2}: (8, {}), {3}: (9, {})} | custom-call | flops 11274289152 | bytes 20000000 | tf_op jit(solution)/shard_map/chunk_1_1/pallas_call | solution.py:250
  110.0 21.7 %chunk_1_2.1 = (bf16[2,3,896,128]{3,2,1,0:T(8,128)(2,1)}, bf16[2,3,896,128]{3,2,1,0:T(8,128)(2,1)}, bf16[2048,2560]{1,0:T(8,128)(2,1)}, bf16[2048,2560]{1,0:T(8,128)(2,1)}, f32[8,128]{1,0:T(8,128)}) custom-call(bf16[2048,896]{1,0:T(8,128)(2,1)} %get-tuple-element.198.refs_0_, ...), custom_call_target="tpu_custom_call", output_to_operand_aliasing={{2}: (8, {}), {3}: (9, {})} | custom-call | flops 11274289152 | bytes 20000000 | tf_op jit(solution)/shard_map/chunk_1_2/pallas_call | solution.py:250
  138.3 12.4 %collective-permute-done.3.refs_2_ = bf16[3,896,128]{2,1,0:T(8,128)(2,1)S(1)} collective-permute-done((bf16[3,896,128]{2,1,0:T(8,128)(2,1)S(1)}, bf16[3,896,128]{2,1,0:T(8,128)(2,1)S(1)}, u32[]{:S(2)}, u32[]{:S(2)}) %collective-permute-start.3) | collective-permute-done | bytes 688160 | tf_op jit(solution)/shard_map/ppermute | solution.py:471
  151.5 6.2 adamw_1_0.1
  157.8 21.2 %chunk_1_3.1 = (bf16[2,3,896,128]{3,2,1,0:T(8,128)(2,1)}, bf16[2,3,896,128]{3,2,1,0:T(8,128)(2,1)}, bf16[2048,2560]{1,0:T(8,128)(2,1)}, bf16[2048,2560]{1,0:T(8,128)(2,1)}, f32[8,128]{1,0:T(8,128)}) custom-call(bf16[2048,896]{1,0:T(8,128)(2,1)} %get-tuple-element.198.refs_0_, ...), custom_call_target="tpu_custom_call", output_to_operand_aliasing={{2}: (8, {}), {3}: (9, {})} | custom-call | flops 11274289152 | bytes 20000000 | tf_op jit(solution)/shard_map/chunk_1_3/pallas_call | solution.py:250
  185.5 11.3 %collective-permute-done.2.refs_2_ = bf16[3,896,128]{2,1,0:T(8,128)(2,1)S(1)} collective-permute-done((bf16[3,896,128]{2,1,0:T(8,128)(2,1)S(1)}, bf16[3,896,128]{2,1,0:T(8,128)(2,1)S(1)}, u32[]{:S(2)}, u32[]{:S(2)}) %collective-permute-start.2) | collective-permute-done | bytes 688160 | tf_op jit(solution)/shard_map/ppermute | solution.py:471
  197.7 6.2 adamw_1_1.1
  203.9 21.3 %chunk_1_4.1 = (bf16[2,3,896,128]{3,2,1,0:T(8,128)(2,1)}, bf16[2,3,896,128]{3,2,1,0:T(8,128)(2,1)}, bf16[2048,2560]{1,0:T(8,128)(2,1)}, bf16[2048,2560]{1,0:T(8,128)(2,1)}, f32[8,128]{1,0:T(8,128)}) custom-call(bf16[2048,896]{1,0:T(8,128)(2,1)} %get-tuple-element.198.refs_0_, ...), custom_call_target="tpu_custom_call", output_to_operand_aliasing={{2}: (8, {}), {3}: (9, {})} | custom-call | flops 11274289152 | bytes 20000000 | tf_op jit(solution)/shard_map/chunk_1_4/pallas_call | solution.py:250
  231.8 11.8 %collective-permute-done.6.refs_2_ = bf16[3,896,128]{2,1,0:T(8,128)(2,1)S(1)} collective-permute-done((bf16[3,896,128]{2,1,0:T(8,128)(2,1)S(1)}, bf16[3,896,128]{2,1,0:T(8,128)(2,1)S(1)}, u32[]{:S(2)}, u32[]{:S(2)}) %collective-permute-start.6) | collective-permute-done | bytes 688160 | tf_op jit(solution)/shard_map/ppermute | solution.py:471
  250.7 32.7 %states_1.1 = (bf16[2048,896]{1,0:T(8,128)(2,1)}, bf16[896,2048]{1,0:T(8,128)(2,1)}, bf16[2048,896]{1,0:T(8,128)(2,1)}, bf16[896,2048]{1,0:T(8,128)(2,1)}, f32[8,128]{1,0:T(8,128)}) custom-call(bf16[2048,2560]{1,0:T(8,128)(2,1)} %get-tuple-element.236.dg, bf16[2048,2560]{1,0:T(8,128)(2,1)} %get-tuple-element.237.du, bf16[2,896,2560]{2,1,0:T(8,128)(2,1)} %refs_3_.19, ...), custom_call_target="tpu_custom_call" | custom-call | flops 18790481920 | bytes 50000000 | tf_op jit(solution)/shard_map/states_1/pallas_call | solution.py:297
  290.5 21.3 %chunk_0_0.1 = (bf16[2,3,896,128]{3,2,1,0:T(8,128)(2,1)}, bf16[2,3,896,128]{3,2,1,0:T(8,128)(2,1)}, f32[8,128]{1,0:T(8,128)}) custom-call(bf16[2048,896]{1,0:T(8,128)(2,1)} %get-tuple-element.251.refs_0_, bf16[896,2048]{1,0:T(8,128)(2,1)} %get-tuple-element.252.refs_1_, bf16[2048,896]{1,0:T(8,128)(2,1)} %get-tuple-element.253.refs_2_, ...), custom_call_target="tpu_custom_call" | custom-call | flops 11274289152 | bytes 20000000 | tf_op jit(solution)/shard_map/chunk_0_0/pallas_call | solution.py:250
  313.9 16.3 %collective-permute-done.12.refs_1_ = bf16[3,896,128]{2,1,0:T(8,128)(2,1)S(1)} collective-permute-done((bf16[3,896,128]{2,1,0:T(8,128)(2,1)S(1)}, bf16[3,896,128]{2,1,0:T(8,128)(2,1)S(1)}, u32[]{:S(2)}, u32[]{:S(2)}) %collective-permute-start.12) | collective-permute-done | bytes 688160 | tf_op jit(solution)/shard_map/ppermute | solution.py:474
  333.6 10.8 %collective-permute-done.15.refs_2_ = bf16[3,896,128]{2,1,0:T(8,128)(2,1)S(1)} collective-permute-done((bf16[3,896,128]{2,1,0:T(8,128)(2,1)S(1)}, bf16[3,896,128]{2,1,0:T(8,128)(2,1)S(1)}, u32[]{:S(2)}, u32[]{:S(2)}) %collective-permute-start.15) | collective-permute-done | bytes 688160 | tf_op jit(solution)/shard_map/ppermute | solution.py:471
  355.3 21.3 %chunk_0_1.1 = (bf16[2,3,896,128]{3,2,1,0:T(8,128)(2,1)}, bf16[2,3,896,128]{3,2,1,0:T(8,128)(2,1)}, f32[8,128]{1,0:T(8,128)}) custom-call(bf16[2048,896]{1,0:T(8,128)(2,1)} %get-tuple-element.251.refs_0_, bf16[896,2048]{1,0:T(8,128)(2,1)} %get-tuple-element.252.refs_1_, bf16[2048,896]{1,0:T(8,128)(2,1)} %get-tuple-element.253.refs_2_, ...), custom_call_target="tpu_custom_call" | custom-call | flops 11274289152 | bytes 20000000 | tf_op jit(solution)/shard_map/chunk_0_1/pallas_call | solution.py:250
  378.6 15.9 %collective-permute-done.23.refs_1_ = bf16[3,896,128]{2,1,0:T(8,128)(2,1)S(1)} collective-permute-done((bf16[3,896,128]{2,1,0:T(8,128)(2,1)S(1)}, bf16[3,896,128]{2,1,0:T(8,128)(2,1)S(1)}, u32[]{:S(2)}, u32[]{:S(2)}) %collective-permute-start.23) | collective-permute-done | bytes 688160 | tf_op jit(solution)/shard_map/ppermute | solution.py:474
  402.8 21.4 %chunk_0_2.1 = (bf16[2,3,896,128]{3,2,1,0:T(8,128)(2,1)}, bf16[2,3,896,128]{3,2,1,0:T(8,128)(2,1)}, f32[8,128]{1,0:T(8,128)}) custom-call(bf16[2048,896]{1,0:T(8,128)(2,1)} %get-tuple-element.251.refs_0_, bf16[896,2048]{1,0:T(8,128)(2,1)} %get-tuple-element.252.refs_1_, bf16[2048,896]{1,0:T(8,128)(2,1)} %get-tuple-element.253.refs_2_, ...), custom_call_target="tpu_custom_call" | custom-call | flops 11274289152 | bytes 20000000 | tf_op jit(solution)/shard_map/chunk_0_2/pallas_call | solution.py:250
  426.7 16.3 %collective-permute-done.19.refs_1_ = bf16[3,896,128]{2,1,0:T(8,128)(2,1)S(1)} collective-permute-done((bf16[3,896,128]{2,1,0:T(8,128)(2,1)S(1)}, bf16[3,896,128]{2,1,0:T(8,128)(2,1)S(1)}, u32[]{:S(2)}, u32[]{:S(2)}) %collective-permute-start.19) | collective-permute-done | bytes 688160 | tf_op jit(solution)/shard_map/ppermute | solution.py:474
  446.4 10.4 %collective-permute-done.22.refs_2_ = bf16[3,896,128]{2,1,0:T(8,128)(2,1)S(1)} collective-permute-done((bf16[3,896,128]{2,1,0:T(8,128)(2,1)}, bf16[3,896,128]{2,1,0:T(8,128)(2,1)S(1)}, u32[]{:S(2)}, u32[]{:S(2)}) %collective-permute-start.22) | collective-permute-done | bytes 688160 | tf_op jit(solution)/shard_map/ppermute | solution.py:471
  468.5 21.2 %chunk_0_3.1 = (bf16[2,3,896,128]{3,2,1,0:T(8,128)(2,1)}, bf16[2,3,896,128]{3,2,1,0:T(8,128)(2,1)}, f32[8,128]{1,0:T(8,128)}) custom-call(bf16[2048,896]{1,0:T(8,128)(2,1)} %get-tuple-element.251.refs_0_, bf16[896,2048]{1,0:T(8,128)(2,1)} %get-tuple-element.252.refs_1_, bf16[2048,896]{1,0:T(8,128)(2,1)} %get-tuple-element.253.refs_2_, ...), custom_call_target="tpu_custom_call" | custom-call | flops 11274289152 | bytes 20000000 | tf_op jit(solution)/shard_map/chunk_0_3/pallas_call | solution.py:250
  491.8 16.3 %collective-permute-done.9.refs_1_ = bf16[3,896,128]{2,1,0:T(8,128)(2,1)S(1)} collective-permute-done((bf16[3,896,128]{2,1,0:T(8,128)(2,1)S(1)}, bf16[3,896,128]{2,1,0:T(8,128)(2,1)S(1)}, u32[]{:S(2)}, u32[]{:S(2)}) %collective-permute-start.9) | collective-permute-done | bytes 688160 | tf_op jit(solution)/shard_map/ppermute | solution.py:474
  511.5 10.8 %collective-permute-done.18.refs_2_ = bf16[3,896,128]{2,1,0:T(8,128)(2,1)S(1)} collective-permute-done((bf16[3,896,128]{2,1,0:T(8,128)(2,1)}, bf16[3,896,128]{2,1,0:T(8,128)(2,1)S(1)}, u32[]{:S(2)}, u32[]{:S(2)}) %collective-permute-start.18) | collective-permute-done | bytes 688160 | tf_op jit(solution)/shard_map/ppermute | solution.py:471
  534.1 21.6 %chunk_0_4.1 = (bf16[2,3,896,128]{3,2,1,0:T(8,128)(2,1)}, bf16[2,3,896,128]{3,2,1,0:T(8,128)(2,1)}, f32[8,128]{1,0:T(8,128)}) custom-call(bf16[2048,896]{1,0:T(8,128)(2,1)} %get-tuple-element.251.refs_0_, bf16[896,2048]{1,0:T(8,128)(2,1)} %get-tuple-element.252.refs_1_, bf16[2048,896]{1,0:T(8,128)(2,1)} %get-tuple-element.253.refs_2_, ...), custom_call_target="tpu_custom_call" | custom-call | flops 11274289152 | bytes 20000000 | tf_op jit(solution)/shard_map/chunk_0_4/pallas_call | solution.py:250
  559.7 14.4 %collective-permute-done.34.refs_1_ = bf16[3,896,128]{2,1,0:T(8,128)(2,1)} collective-permute-done((bf16[3,896,128]{2,1,0:T(8,128)(2,1)S(1)}, bf16[3,896,128]{2,1,0:T(8,128)(2,1)}, u32[]{:S(2)}, u32[]{:S(2)}) %collective-permute-start.34) | collective-permute-done | bytes 688160 | tf_op jit(solution)/shard_map/ppermute | solution.py:474
  580.0 8.7 %collective-permute-done.37.refs_2_ = bf16[3,896,128]{2,1,0:T(8,128)(2,1)S(1)} collective-permute-done((bf16[3,896,128]{2,1,0:T(8,128)(2,1)}, bf16[3,896,128]{2,1,0:T(8,128)(2,1)S(1)}, u32[]{:S(2)}, u32[]{:S(2)}) %collective-permute-start.37) | collective-permute-done | bytes 688160 | tf_op jit(solution)/shard_map/ppermute | solution.py:471
  588.8 14.7 %collective-permute-done.30.refs_1_ = bf16[3,896,128]{2,1,0:T(8,128)(2,1)} collective-permute-done((bf16[3,896,128]{2,1,0:T(8,128)(2,1)}, bf16[3,896,128]{2,1,0:T(8,128)(2,1)}, u32[]{:S(2)}, u32[]{:S(2)}) %collective-permute-start.30) | collective-permute-done | bytes 688160 | tf_op jit(solution)/shard_map/ppermute | solution.py:474
  603.5 6.2 adamw_0_2.1
  618.3 14.7 %collective-permute-done.47.refs_1_ = bf16[3,896,128]{2,1,0:T(8,128)(2,1)S(1)} collective-permute-done((bf16[3,896,128]{2,1,0:T(8,128)(2,1)S(1)}, bf16[3,896,128]{2,1,0:T(8,128)(2,1)S(1)}, u32[]{:S(2)}, u32[]{:S(2)}) %collective-permute-start.47) | collective-permute-done | bytes 688160 | tf_op jit(solution)/shard_map/ppermute | solution.py:474
  633.0 6.5 adamw_0_3.1
  663.0 14.2 %collective-permute-done.41.refs_1_ = bf16[3,896,128]{2,1,0:T(8,128)(2,1)} collective-permute-done((bf16[3,896,128]{2,1,0:T(8,128)(2,1)S(1)}, bf16[3,896,128]{2,1,0:T(8,128)(2,1)}, u32[]{:S(2)}, u32[]{:S(2)}) %collective-permute-start.41) | collective-permute-done | bytes 688160 | tf_op jit(solution)/shard_map/ppermute | solution.py:474
  677.8 13.7 %collective-permute-done.38.refs_1_ = bf16[3,896,128]{2,1,0:T(8,128)(2,1)S(1)} collective-permute-done((bf16[3,896,128]{2,1,0:T(8,128)(2,1)}, bf16[3,896,128]{2,1,0:T(8,128)(2,1)S(1)}, u32[]{:S(2)}, u32[]{:S(2)}) %collective-permute-start.38) | collective-permute-done | bytes 688160 | tf_op jit(solution)/shard_map/ppermute | solution.py:474
  (206 shorter events, 170.0 us)
Async XLA Ops:
  132.1 18.6 %collective-permute-start.3 = (bf16[3,896,128]{2,1,0:T(8,128)(2,1)S(1)}, bf16[3,896,128]{2,1,0:T(8,128)(2,1)S(1)}, u32[]{:S(2)}, u32[]{:S(2)}) collective-permute-start(bf16[3,896,128]{2,1,0:T(8,128)(2,1)S(1)} %copy-done.47), channel_id=1, source_target_pairs={{0,2},{1,3},{2,0},{3,1},{4,6},{5,7},{6,4},{7,5}} | collective-permute-start | bytes 2064392 | tf_op jit(solution)/shard_map/ppermute | solution.py:471
  227.1 56.3 %collective-permute-start.8 = (bf16[3,896,128]{2,1,0:T(8,128)(2,1)S(1)}, bf16[3,896,128]{2,1,0:T(8,128)(2,1)S(1)}, u32[]{:S(2)}, u32[]{:S(2)}) collective-permute-start(bf16[3,896,128]{2,1,0:T(8,128)(2,1)S(1)} %copy-done.44), channel_id=1, source_target_pairs={{0,2},{1,3},{2,0},{3,1},{4,6},{5,7},{6,4},{7,5}} | collective-permute-start | bytes 2064392 | tf_op jit(solution)/shard_map/ppermute | solution.py:471
  313.6 30.8 %collective-permute-start.15 = (bf16[3,896,128]{2,1,0:T(8,128)(2,1)S(1)}, bf16[3,896,128]{2,1,0:T(8,128)(2,1)S(1)}, u32[]{:S(2)}, u32[]{:S(2)}) collective-permute-start(bf16[3,896,128]{2,1,0:T(8,128)(2,1)S(1)} %copy-done.43), channel_id=1, source_target_pairs={{0,2},{1,3},{2,0},{3,1},{4,6},{5,7},{6,4},{7,5}} | collective-permute-start | bytes 2064392 | tf_op jit(solution)/shard_map/ppermute | solution.py:471
  313.9 37.6 %collective-permute-start.13 = (bf16[3,896,128]{2,1,0:T(8,128)(2,1)S(1)}, bf16[3,896,128]{2,1,0:T(8,128)(2,1)}, u32[]{:S(2)}, u32[]{:S(2)}) collective-permute-start(bf16[3,896,128]{2,1,0:T(8,128)(2,1)S(1)} %copy-done.41), channel_id=1, source_target_pairs={{0,1},{1,0},{2,3},{3,2},{4,5},{5,4},{6,7},{7,6}} | collective-permute-start | bytes 2064392 | tf_op jit(solution)/shard_map/ppermute | solution.py:475
  330.2 21.3 %collective-permute-start.14 = (bf16[3,896,128]{2,1,0:T(8,128)(2,1)S(1)}, bf16[3,896,128]{2,1,0:T(8,128)(2,1)}, u32[]{:S(2)}, u32[]{:S(2)}) collective-permute-start(bf16[3,896,128]{2,1,0:T(8,128)(2,1)S(1)} %collective-permute-done.12.refs_1_), channel_id=1, source_target_pairs={{0,1},{1,0},{2,3},{3,2},{4,5},{5,4},{6,7},{7,6}} | collective-permute-start | bytes 2064392 | tf_op jit(solution)/shard_map/ppermute | solution.py:475
  378.4 19.5 %collective-permute-start.24 = (bf16[3,896,128]{2,1,0:T(8,128)(2,1)S(1)}, bf16[3,896,128]{2,1,0:T(8,128)(2,1)S(1)}, u32[]{:S(2)}, u32[]{:S(2)}) collective-permute-start(bf16[3,896,128]{2,1,0:T(8,128)(2,1)S(1)} %copy-done.23), channel_id=1, source_target_pairs={{0,1},{1,0},{2,3},{3,2},{4,5},{5,4},{6,7},{7,6}} | collective-permute-start | bytes 2064392 | tf_op jit(solution)/shard_map/ppermute | solution.py:475
  424.2 18.8 %collective-permute-start.26 = (bf16[2,3,896,128]{3,2,1,0:T(8,128)(2,1)}, bf16[2,3,896,128]{3,2,1,0:T(8,128)(2,1)S(1)}, u32[]{:S(2)}, u32[]{:S(2)}) collective-permute-start(bf16[2,3,896,128]{3,2,1,0:T(8,128)(2,1)} %get-tuple-element.292), channel_id=1, source_target_pairs={{0,1},{1,0},{2,3},{3,2},{4,5},{5,4},{6,7},{7,6}} | collective-permute-start | bytes 4128776 | tf_op jit(solution)/shard_map/ppermute | solution.py:468
  426.4 30.4 %collective-permute-start.22 = (bf16[3,896,128]{2,1,0:T(8,128)(2,1)}, bf16[3,896,128]{2,1,0:T(8,128)(2,1)S(1)}, u32[]{:S(2)}, u32[]{:S(2)}) collective-permute-start(bf16[3,896,128]{2,1,0:T(8,128)(2,1)} %get-tuple-element.284), channel_id=1, source_target_pairs={{0,2},{1,3},{2,0},{3,1},{4,6},{5,7},{6,4},{7,5}} | collective-permute-start | bytes 2064392 | tf_op jit(solution)/shard_map/ppermute | solution.py:471
  426.7 37.2 %collective-permute-start.20 = (bf16[3,896,128]{2,1,0:T(8,128)(2,1)S(1)}, bf16[3,896,128]{2,1,0:T(8,128)(2,1)S(1)}, u32[]{:S(2)}, u32[]{:S(2)}) collective-permute-start(bf16[3,896,128]{2,1,0:T(8,128)(2,1)S(1)} %copy-done.22), channel_id=1, source_target_pairs={{0,1},{1,0},{2,3},{3,2},{4,5},{5,4},{6,7},{7,6}} | collective-permute-start | bytes 2064392 | tf_op jit(solution)/shard_map/ppermute | solution.py:475
  443.0 20.9 %collective-permute-start.21 = (bf16[3,896,128]{2,1,0:T(8,128)(2,1)S(1)}, bf16[3,896,128]{2,1,0:T(8,128)(2,1)}, u32[]{:S(2)}, u32[]{:S(2)}) collective-permute-start(bf16[3,896,128]{2,1,0:T(8,128)(2,1)S(1)} %collective-permute-done.19.refs_1_), channel_id=1, source_target_pairs={{0,1},{1,0},{2,3},{3,2},{4,5},{5,4},{6,7},{7,6}} | collective-permute-start | bytes 2064392 | tf_op jit(solution)/shard_map/ppermute | solution.py:475
  491.5 30.8 %collective-permute-start.18 = (bf16[3,896,128]{2,1,0:T(8,128)(2,1)}, bf16[3,896,128]{2,1,0:T(8,128)(2,1)S(1)}, u32[]{:S(2)}, u32[]{:S(2)}) collective-permute-start(bf16[3,896,128]{2,1,0:T(8,128)(2,1)} %get-tuple-element.282), channel_id=1, source_target_pairs={{0,2},{1,3},{2,0},{3,1},{4,6},{5,7},{6,4},{7,5}} | collective-permute-start | bytes 2064392 | tf_op jit(solution)/shard_map/ppermute | solution.py:471
  491.8 37.6 %collective-permute-start.10 = (bf16[3,896,128]{2,1,0:T(8,128)(2,1)S(1)}, bf16[3,896,128]{2,1,0:T(8,128)(2,1)S(1)}, u32[]{:S(2)}, u32[]{:S(2)}) collective-permute-start(bf16[3,896,128]{2,1,0:T(8,128)(2,1)S(1)} %copy-done.20), channel_id=1, source_target_pairs={{0,1},{1,0},{2,3},{3,2},{4,5},{5,4},{6,7},{7,6}} | collective-permute-start | bytes 2064392 | tf_op jit(solution)/shard_map/ppermute | solution.py:475
  508.1 21.4 %collective-permute-start.11 = (bf16[3,896,128]{2,1,0:T(8,128)(2,1)S(1)}, bf16[3,896,128]{2,1,0:T(8,128)(2,1)}, u32[]{:S(2)}, u32[]{:S(2)}) collective-permute-start(bf16[3,896,128]{2,1,0:T(8,128)(2,1)S(1)} %collective-permute-done.9.refs_1_), channel_id=1, source_target_pairs={{0,1},{1,0},{2,3},{3,2},{4,5},{5,4},{6,7},{7,6}} | collective-permute-start | bytes 2064392 | tf_op jit(solution)/shard_map/ppermute | solution.py:475
  555.7 21.0 %collective-permute-start.28 = (bf16[2,3,896,128]{3,2,1,0:T(8,128)(2,1)}, bf16[2,3,896,128]{3,2,1,0:T(8,128)(2,1)S(1)}, u32[]{:S(2)}, u32[]{:S(2)}) collective-permute-start(bf16[2,3,896,128]{3,2,1,0:T(8,128)(2,1)} %get-tuple-element.322), channel_id=1, source_target_pairs={{0,1},{1,0},{2,3},{3,2},{4,5},{5,4},{6,7},{7,6}} | collective-permute-start | bytes 4128776 | tf_op jit(solution)/shard_map/ppermute | solution.py:468
  557.7 31.1 %collective-permute-start.37 = (bf16[3,896,128]{2,1,0:T(8,128)(2,1)}, bf16[3,896,128]{2,1,0:T(8,128)(2,1)S(1)}, u32[]{:S(2)}, u32[]{:S(2)}) collective-permute-start(bf16[3,896,128]{2,1,0:T(8,128)(2,1)} %get-tuple-element.328), channel_id=1, source_target_pairs={{0,2},{1,3},{2,0},{3,1},{4,6},{5,7},{6,4},{7,5}} | collective-permute-start | bytes 2064392 | tf_op jit(solution)/shard_map/ppermute | solution.py:471
  557.9 45.6 %collective-permute-start.30 = (bf16[3,896,128]{2,1,0:T(8,128)(2,1)}, bf16[3,896,128]{2,1,0:T(8,128)(2,1)}, u32[]{:S(2)}, u32[]{:S(2)}) collective-permute-start(bf16[3,896,128]{2,1,0:T(8,128)(2,1)} %get-tuple-element.325.refs_0_), channel_id=1, source_target_pairs={{0,2},{1,3},{2,0},{3,1},{4,6},{5,7},{6,4},{7,5}} | collective-permute-start | bytes 2064392 | tf_op jit(solution)/shard_map/ppermute | solution.py:474
  574.0 35.7 %collective-permute-start.36 = (bf16[3,896,128]{2,1,0:T(8,128)(2,1)}, bf16[3,896,128]{2,1,0:T(8,128)(2,1)}, u32[]{:S(2)}, u32[]{:S(2)}) collective-permute-start(bf16[3,896,128]{2,1,0:T(8,128)(2,1)} %collective-permute-done.34.refs_1_), channel_id=1, source_target_pairs={{0,1},{1,0},{2,3},{3,2},{4,5},{5,4},{6,7},{7,6}} | collective-permute-start | bytes 2064392 | tf_op jit(solution)/shard_map/ppermute | solution.py:475
  574.9 43.4 %collective-permute-start.33 = (bf16[3,896,128]{2,1,0:T(8,128)(2,1)}, bf16[3,896,128]{2,1,0:T(8,128)(2,1)S(1)}, u32[]{:S(2)}, u32[]{:S(2)}) collective-permute-start(bf16[3,896,128]{2,1,0:T(8,128)(2,1)} %get-tuple-element.326), channel_id=1, source_target_pairs={{0,2},{1,3},{2,0},{3,1},{4,6},{5,7},{6,4},{7,5}} | collective-permute-start | bytes 2064392 | tf_op jit(solution)/shard_map/ppermute | solution.py:471
  576.6 56.4 %collective-permute-start.47 = (bf16[3,896,128]{2,1,0:T(8,128)(2,1)S(1)}, bf16[3,896,128]{2,1,0:T(8,128)(2,1)S(1)}, u32[]{:S(2)}, u32[]{:S(2)}) collective-permute-start(bf16[3,896,128]{2,1,0:T(8,128)(2,1)S(1)} %copy-done.21), channel_id=1, source_target_pairs={{0,2},{1,3},{2,0},{3,1},{4,6},{5,7},{6,4},{7,5}} | collective-permute-start | bytes 2064392 | tf_op jit(solution)/shard_map/ppermute | solution.py:474
  588.8 50.8 %collective-permute-start.31 = (bf16[3,896,128]{2,1,0:T(8,128)(2,1)}, bf16[3,896,128]{2,1,0:T(8,128)(2,1)}, u32[]{:S(2)}, u32[]{:S(2)}) collective-permute-start(bf16[3,896,128]{2,1,0:T(8,128)(2,1)} %get-tuple-element.325.refs_0_), channel_id=1, source_target_pairs={{0,1},{1,0},{2,3},{3,2},{4,5},{5,4},{6,7},{7,6}} | collective-permute-start | bytes 2064392 | tf_op jit(solution)/shard_map/ppermute | solution.py:475
  603.5 37.8 %collective-permute-start.32 = (bf16[3,896,128]{2,1,0:T(8,128)(2,1)}, bf16[3,896,128]{2,1,0:T(8,128)(2,1)}, u32[]{:S(2)}, u32[]{:S(2)}) collective-permute-start(bf16[3,896,128]{2,1,0:T(8,128)(2,1)} %collective-permute-done.30.refs_1_), channel_id=1, source_target_pairs={{0,1},{1,0},{2,3},{3,2},{4,5},{5,4},{6,7},{7,6}} | collective-permute-start | bytes 2064392 | tf_op jit(solution)/shard_map/ppermute | solution.py:475
  609.8 38.0 %collective-permute-start.29 = (bf16[3,896,128]{2,1,0:T(8,128)(2,1)}, bf16[3,896,128]{2,1,0:T(8,128)(2,1)S(1)}, u32[]{:S(2)}, u32[]{:S(2)}) collective-permute-start(bf16[3,896,128]{2,1,0:T(8,128)(2,1)} %get-tuple-element.324), channel_id=1, source_target_pairs={{0,2},{1,3},{2,0},{3,1},{4,6},{5,7},{6,4},{7,5}} | collective-permute-start | bytes 2064392 | tf_op jit(solution)/shard_map/ppermute | solution.py:471
  618.3 37.4 %collective-permute-start.48 = (bf16[3,896,128]{2,1,0:T(8,128)(2,1)S(1)}, bf16[3,896,128]{2,1,0:T(8,128)(2,1)S(1)}, u32[]{:S(2)}, u32[]{:S(2)}) collective-permute-start(bf16[3,896,128]{2,1,0:T(8,128)(2,1)S(1)} %copy-done.21), channel_id=1, source_target_pairs={{0,1},{1,0},{2,3},{3,2},{4,5},{5,4},{6,7},{7,6}} | collective-permute-start | bytes 2064392 | tf_op jit(solution)/shard_map/ppermute | solution.py:475
  633.0 29.5 %collective-permute-start.49 = (bf16[3,896,128]{2,1,0:T(8,128)(2,1)S(1)}, bf16[3,896,128]{2,1,0:T(8,128)(2,1)}, u32[]{:S(2)}, u32[]{:S(2)}) collective-permute-start(bf16[3,896,128]{2,1,0:T(8,128)(2,1)S(1)} %collective-permute-done.47.refs_1_), channel_id=1, source_target_pairs={{0,1},{1,0},{2,3},{3,2},{4,5},{5,4},{6,7},{7,6}} | collective-permute-start | bytes 2064392 | tf_op jit(solution)/shard_map/ppermute | solution.py:475
  639.6 22.9 %collective-permute-start.44 = (bf16[3,896,128]{2,1,0:T(8,128)(2,1)S(1)}, bf16[3,896,128]{2,1,0:T(8,128)(2,1)}, u32[]{:S(2)}, u32[]{:S(2)}) collective-permute-start(bf16[3,896,128]{2,1,0:T(8,128)(2,1)S(1)} %copy-done.25), channel_id=1, source_target_pairs={{0,2},{1,3},{2,0},{3,1},{4,6},{5,7},{6,4},{7,5}} | collective-permute-start | bytes 2064392 | tf_op jit(solution)/shard_map/ppermute | solution.py:474
  641.3 35.9 %collective-permute-start.45 = (bf16[3,896,128]{2,1,0:T(8,128)(2,1)S(1)}, bf16[3,896,128]{2,1,0:T(8,128)(2,1)}, u32[]{:S(2)}, u32[]{:S(2)}) collective-permute-start(bf16[3,896,128]{2,1,0:T(8,128)(2,1)S(1)} %copy-done.25), channel_id=1, source_target_pairs={{0,1},{1,0},{2,3},{3,2},{4,5},{5,4},{6,7},{7,6}} | collective-permute-start | bytes 2064392 | tf_op jit(solution)/shard_map/ppermute | solution.py:475
  647.8 29.5 %collective-permute-start.41 = (bf16[3,896,128]{2,1,0:T(8,128)(2,1)S(1)}, bf16[3,896,128]{2,1,0:T(8,128)(2,1)}, u32[]{:S(2)}, u32[]{:S(2)}) collective-permute-start(bf16[3,896,128]{2,1,0:T(8,128)(2,1)S(1)} %copy-done.26), channel_id=1, source_target_pairs={{0,2},{1,3},{2,0},{3,1},{4,6},{5,7},{6,4},{7,5}} | collective-permute-start | bytes 2064392 | tf_op jit(solution)/shard_map/ppermute | solution.py:474
  655.7 35.8 %collective-permute-start.38 = (bf16[3,896,128]{2,1,0:T(8,128)(2,1)}, bf16[3,896,128]{2,1,0:T(8,128)(2,1)S(1)}, u32[]{:S(2)}, u32[]{:S(2)}) collective-permute-start(bf16[3,896,128]{2,1,0:T(8,128)(2,1)} %get-tuple-element.358.refs_0_), channel_id=1, source_target_pairs={{0,2},{1,3},{2,0},{3,1},{4,6},{5,7},{6,4},{7,5}} | collective-permute-start | bytes 2064392 | tf_op jit(solution)/shard_map/ppermute | solution.py:474
  662.5 33.0 %collective-permute-start.46 = (bf16[3,896,128]{2,1,0:T(8,128)(2,1)}, bf16[3,896,128]{2,1,0:T(8,128)(2,1)}, u32[]{:S(2)}, u32[]{:S(2)}) collective-permute-start(bf16[3,896,128]{2,1,0:T(8,128)(2,1)} %collective-permute-done.44.refs_1_), channel_id=1, source_target_pairs={{0,1},{1,0},{2,3},{3,2},{4,5},{5,4},{6,7},{7,6}} | collective-permute-start | bytes 2064392 | tf_op jit(solution)/shard_map/ppermute | solution.py:475
  662.5 36.8 %collective-permute-start.42 = (bf16[3,896,128]{2,1,0:T(8,128)(2,1)S(1)}, bf16[3,896,128]{2,1,0:T(8,128)(2,1)S(1)}, u32[]{:S(2)}, u32[]{:S(2)}) collective-permute-start(bf16[3,896,128]{2,1,0:T(8,128)(2,1)S(1)} %copy-done.26), channel_id=1, source_target_pairs={{0,1},{1,0},{2,3},{3,2},{4,5},{5,4},{6,7},{7,6}} | collective-permute-start | bytes 2064392 | tf_op jit(solution)/shard_map/ppermute | solution.py:475
  677.3 22.1 %collective-permute-start.43 = (bf16[3,896,128]{2,1,0:T(8,128)(2,1)}, bf16[3,896,128]{2,1,0:T(8,128)(2,1)}, u32[]{:S(2)}, u32[]{:S(2)}) collective-permute-start(bf16[3,896,128]{2,1,0:T(8,128)(2,1)} %collective-permute-done.41.refs_1_), channel_id=1, source_target_pairs={{0,1},{1,0},{2,3},{3,2},{4,5},{5,4},{6,7},{7,6}} | collective-permute-start | bytes 2064392 | tf_op jit(solution)/shard_map/ppermute | solution.py:475
  677.3 26.7 %collective-permute-start.39 = (bf16[3,896,128]{2,1,0:T(8,128)(2,1)}, bf16[3,896,128]{2,1,0:T(8,128)(2,1)S(1)}, u32[]{:S(2)}, u32[]{:S(2)}) collective-permute-start(bf16[3,896,128]{2,1,0:T(8,128)(2,1)} %get-tuple-element.358.refs_0_), channel_id=1, source_target_pairs={{0,1},{1,0},{2,3},{3,2},{4,5},{5,4},{6,7},{7,6}} | collective-permute-start | bytes 2064392 | tf_op jit(solution)/shard_map/ppermute | solution.py:475
  (66 other events, 673.6 us)
